TPU v7x, 32 devices: a whole 2x2x4 slice. The times are simulated.
32 devices in a mesh: beam: 2 (over x), fft: 16 (over z, y, core).
Axes of the slice: x: 2, y: 2, z: 4, core: 2. Of those that a mesh axis runs over, the one named last changes fastest.
Arguments:
- baseband: bfloat16 [4, 33554432], P('beam', 'fft'), parts along dimension 0, may hold values from -6 to 6
- spectrum_in: bfloat16 [4, 4096, 8192], P('beam', 'fft'), parts along dimension 0, may hold values from -6 to 6
- dm_index: int32 [1], replicated, may hold values from 0 to 63
Outputs:
- spectrum_out: bfloat16 [4, 4096, 8192], P('beam', 'fft'), parts along dimension 0
- smoothed: float32 [2, 2097152], P('beam', 'fft'), parts along dimension 0
There are 2 independent parts, one for each index of `beam`. A program takes and returns all parts, laid end to end along the dimension named above; an argument that names none is the same for every part. Nothing has to cross between parts.
Inputs may be any that keep to these rules, and one draw needn't show every extreme that they name: `dm_index`: indices into the grid of 64 trial dispersion measures.
All inputs are finite; a program needn't handle non-finite values.
Results may differ from a plain program's by a relative error of at most 0.0019.
The roundings to bfloat16 on the way count: a program that leaves them out, or rounds other values in their place, can miss the bound.
Values may be sent and summed in bfloat16 or wider, within the bound.
A program may use at most 128 MiB of HBM per device.

v0:
```python
import math
import jax
import jax.numpy as jnp
from jax import lax
from jax.sharding import PartitionSpec as P

ROWS_OUTER = 32
ROWS_INNER = 128
COLS_OUTER = 64
COLS_INNER = 128
ROW_LENGTH = 4096
COLUMN_LENGTH = 8192
SEGMENT_SAMPLES = 33554432
DM_GRID = 64
DECIMATE_FACTOR = 16
HALF_WIDTH = 16


def padded_2(block, sides, width):
    for axis, dim in sides:
        count = lax.axis_size(axis)
        forward = [(i, i + 1) for i in range(count - 1)]
        backward = [(target, source) for source, target in forward]
        low = lax.ppermute(
            lax.slice_in_dim(block, block.shape[dim] - width, None, axis=dim), axis, forward
        )
        high = lax.ppermute(lax.slice_in_dim(block, 0, width, axis=dim), axis, backward)
        block = jnp.concatenate([low, block, high], axis=dim)
    return block


def dft_table(length, direction):
    positions = jnp.arange(length, dtype=jnp.int32)
    product = jnp.remainder(positions[:, None] * positions[None, :], length)
    radians = direction * 2.0 * math.pi / length * product.astype(jnp.float32)
    norm_scale = 1.0 / math.sqrt(length)
    cosine = jnp.cos(radians) * norm_scale
    sine_part = jnp.sin(radians) * norm_scale
    return jnp.stack([jnp.stack([cosine, sine_part]), jnp.stack([-sine_part, cosine])]).astype(
        jnp.bfloat16
    )


def radians_of(numer, modulus, direction):
    return direction * 2.0 * math.pi / modulus * jnp.remainder(numer, modulus).astype(jnp.float32)


def chirp_radians(freq_row, col_outer, col_inner, grid_steps):
    col_freq = col_outer + COLS_OUTER * col_inner
    whole_mod = 4.0 * DM_GRID * ROW_LENGTH * COLUMN_LENGTH
    cross_mod = 2 * DM_GRID * COLUMN_LENGTH
    square_mod = 4 * DM_GRID * COLUMN_LENGTH
    grid_float = grid_steps.astype(jnp.float32)
    row_square = (freq_row * freq_row).astype(jnp.float32)
    term_rows = grid_float[:, None, None, None] * row_square[None, :, None, None] / whole_mod
    cross = jnp.remainder(freq_row[:, None, None] * col_freq[None], cross_mod)
    cross = jnp.remainder(grid_steps[:, None, None, None] * cross[None], cross_mod)
    square = jnp.remainder(col_freq * col_freq, square_mod)
    square = jnp.remainder(grid_steps[:, None, None] * square[None], square_mod)
    high_part = square // 512
    low_part = square % 512
    square = jnp.remainder(
        jnp.remainder(ROW_LENGTH * high_part, square_mod) * 512 + ROW_LENGTH * low_part, square_mod
    )
    turns = (
        term_rows
        + cross.astype(jnp.float32) / cross_mod
        + square[:, None].astype(jnp.float32) / square_mod
    )
    return 2.0 * math.pi * turns


def rotate(values, radians):
    cosine = jnp.cos(radians)
    sine_part = jnp.sin(radians)
    real_part = values[:, 0] * cosine - values[:, 1] * sine_part
    imag_part = values[:, 0] * sine_part + values[:, 1] * cosine
    return jnp.stack([real_part, imag_part], axis=1).astype(jnp.bfloat16)


def dft_section(values, einsum_form, length, direction, radians):
    mixed_sum = jnp.einsum(
        einsum_form, values, dft_table(length, direction), preferred_element_type=jnp.float32
    )
    if radians is None:
        return mixed_sum.astype(jnp.bfloat16)
    return rotate(mixed_sum, radians)


def row_frequency(row_pos):
    return row_pos // ROWS_INNER + ROWS_OUTER * (row_pos % ROWS_INNER)


def chirp_front(spectrum, grid_steps, row_start, row_local):
    trial_total = grid_steps.shape[0]
    row_pos = row_start + jnp.arange(row_local, dtype=jnp.int32)
    freq_row = row_frequency(row_pos)
    col_outer = jnp.arange(COLS_OUTER, dtype=jnp.int32)[:, None]
    col_inner = jnp.arange(COLS_INNER, dtype=jnp.int32)[None, :]
    values = rotate(
        spectrum.astype(jnp.float32).reshape(1, 2, row_local, COLS_OUTER, COLS_INNER),
        chirp_radians(freq_row, col_outer, col_inner, grid_steps),
    )
    values = dft_section(
        values,
        "dimjq,ioqy->domjy",
        COLS_INNER,
        1,
        radians_of(col_outer * col_inner, COLUMN_LENGTH, 1),
    )
    col_time = COLS_INNER * col_outer + col_inner
    values = dft_section(
        values,
        "dimjy,iojx->domxy",
        COLS_OUTER,
        1,
        radians_of(freq_row[:, None, None] * col_time[None], SEGMENT_SAMPLES, 1),
    )
    return values.reshape(trial_total, 2, row_local, COLUMN_LENGTH)


def finish_rows(values):
    trial_total = values.shape[0]
    col_local = values.shape[3]
    values = values.reshape(trial_total, 2, ROWS_OUTER, ROWS_INNER, col_local)
    outer_pos = jnp.arange(ROWS_OUTER, dtype=jnp.int32)[:, None]
    inner_pos = jnp.arange(ROWS_INNER, dtype=jnp.int32)[None, :]
    values = dft_section(
        values,
        "dikqb,ioqy->dokyb",
        ROWS_INNER,
        1,
        radians_of(outer_pos * inner_pos, ROW_LENGTH, 1)[:, :, None],
    )
    values = dft_section(values, "dikyb,iokx->doxyb", ROWS_OUTER, 1, None)
    return values.reshape(trial_total, 2, ROW_LENGTH, col_local)


def detect(values):
    trial_total = values.shape[0]
    row_total = values.shape[2]
    column_total = values.shape[3]
    wide = values.astype(jnp.float32)
    detected_power = wide[:, 0] * wide[:, 0] + wide[:, 1] * wide[:, 1]
    return jnp.mean(
        detected_power.reshape(
            trial_total, row_total, column_total // DECIMATE_FACTOR, DECIMATE_FACTOR
        ),
        axis=3,
    )


def on_device(baseband, spectrum_in, dm_index):
    device_index = lax.axis_index("fft")
    row_local = spectrum_in.shape[1]
    col_local = COLUMN_LENGTH // (ROW_LENGTH // row_local)
    values = baseband.reshape(2, row_local, COLUMN_LENGTH)
    values = lax.all_to_all(values, "fft", split_axis=2, concat_axis=1, tiled=True)
    values = values.reshape(1, 2, ROWS_OUTER, ROWS_INNER, col_local)
    outer_pos = jnp.arange(ROWS_OUTER, dtype=jnp.int32)[:, None]
    inner_pos = jnp.arange(ROWS_INNER, dtype=jnp.int32)[None, :]
    values = dft_section(
        values,
        "dixyb,ioxk->dokyb",
        ROWS_OUTER,
        -1,
        radians_of(outer_pos * inner_pos, ROW_LENGTH, -1)[:, :, None],
    )
    freq_row = outer_pos + ROWS_OUTER * inner_pos
    col_pos = device_index * col_local + jnp.arange(col_local, dtype=jnp.int32)
    values = dft_section(
        values,
        "dikyb,ioyq->dokqb",
        ROWS_INNER,
        -1,
        radians_of(freq_row[:, :, None] * col_pos[None, None, :], SEGMENT_SAMPLES, -1),
    )
    values = values.reshape(1, 2, ROW_LENGTH, col_local)
    values = lax.all_to_all(values, "fft", split_axis=2, concat_axis=3, tiled=True)
    values = values.reshape(1, 2, row_local, COLS_OUTER, COLS_INNER)
    col_outer = jnp.arange(COLS_OUTER, dtype=jnp.int32)[:, None]
    col_inner = jnp.arange(COLS_INNER, dtype=jnp.int32)[None, :]
    values = dft_section(
        values,
        "dimxy,ioxj->domjy",
        COLS_OUTER,
        -1,
        radians_of(col_outer * col_inner, COLUMN_LENGTH, -1),
    )
    values = dft_section(values, "dimjy,ioyq->domjq", COLS_INNER, -1, None)
    spectrum_out = values[0].reshape(2, row_local, COLUMN_LENGTH)
    grid_steps = dm_index + 1
    row_start = device_index * row_local
    trial_total = dm_index.shape[0]
    front_part = chirp_front(spectrum_in, grid_steps, row_start, row_local)
    moved = lax.all_to_all(front_part, "fft", split_axis=3, concat_axis=2, tiled=True)
    pieces = finish_rows(moved)
    decimated_power = lax.all_to_all(
        detect(pieces).astype(jnp.bfloat16), "fft", split_axis=1, concat_axis=2, tiled=True
    ).astype(jnp.float32)
    series = decimated_power.reshape(
        trial_total, decimated_power.shape[1] * decimated_power.shape[2]
    )
    padded = padded_2(series.astype(jnp.bfloat16), (("fft", 1),), HALF_WIDTH).astype(series.dtype)
    length = series.shape[1]
    window_sum = padded[:, 0:length]
    for offset in range(1, 2 * HALF_WIDTH + 1):
        window_sum = window_sum + padded[:, offset : offset + length]
    smoothed = window_sum / (2 * HALF_WIDTH + 1)
    return (spectrum_out, smoothed)


def solution(mesh):
    placed = (P("beam", "fft"), P("beam", "fft", None), P())
    return jax.shard_map(
        on_device,
        mesh=mesh,
        in_specs=placed,
        out_specs=(P("beam", "fft", None), P("beam", "fft")),
        check_vma=False,
    )
```

profile of v0, /device:TPU:16, one launch (start us, length us, event | category | flops | bytes accessed | tf_op | source)
XLA Modules:
  0.0 1084.0 jit_solution(8108217904448306539)
XLA Ops:
  2.5 11.9 %copy.194 = bf16[2,256,8192]{1,2,0:T(8,128)(2,1)} copy(bf16[2,256,8192]{2,1,0:T(8,128)(2,1)} %param.4) | data formatting | bytes 16777216 | tf_op args[1]
  14.4 11.5 %fusion.129 = (f32[1,1,256,64,128]{2,4,3,1,0:T(8,128)}, f32[1,1,256,64,128]{2,4,3,1,0:T(8,128)}) fusion(bf16[1,2,256,64,128]{2,4,3,1,0:T(8,128)(2,1)} %bitcast.212), kind=kLoop, calls=%fused_computation.287 | loop fusion | bytes 33554432 | tf_op jit(solution)/shard_map/slice | solution.py:76
  26.0 9.0 copy.240
  35.0 9.0 copy.241
  44.0 41.0 %fusion.57 = (bf16[1,256,64,128]{3,1,0,2:T(8,128)(2,1)S(1)}, bf16[1,256,64,128]{3,1,0,2:T(8,128)(2,1)S(1)}) fusion(f32[1,1,256,64,128]{4,2,3,1,0:T(8,128)} %copy.241, f32[1,1,256,64,128]{4,2,3,1,0:T(8,128)} %copy.240, f32[64,128]{1,0:T(8,128)S(1)} %fusion.97, s32[64,128]{1,0:T(8,128)S(1)} %iota_add_fusion.1, s32[256]{0:T(256)S(1)} %fusion.122, s32[]{:T(128)} %bitcast.60, ...), kind=kLoop, calls=%fused_computation.92 | loop fusion | flops 77594624 | bytes 25233412 | tf_op jit(solution)/shard_map/stack | solution.py:78
  85.0 7.0 fusion.47
  92.0 8.8 fusion.59
  100.8 6.3 pad_maximum_fusion.3
  107.2 12.2 %copy.200 = bf16[2,256,64,128]{3,2,0,1:T(8,128)(2,1)} copy(bf16[2,256,64,128]{1,3,2,0:T(8,128)(2,1)} %pad_maximum_fusion.3) | data formatting | bytes 16777216 | tf_op jit(solution)/shard_map/stack | solution.py:78
  119.4 5.8 fusion.48
  125.2 18.3 %copy.285 = f32[2,64,256,128]{3,2,1,0:T(8,128)S(1)} copy(f32[2,64,256,128]{3,1,2,0:T(8,128)S(1)} %fusion.48) | data formatting | bytes 33554432 | tf_op jit(solution)/shard_map/dimjy,iojx->domxy/dot_general | solution.py:82
  143.6 37.2 %subtract_convert_fusion.1 = (bf16[1,1,256,64,128]{4,2,3,1,0:T(8,128)(2,1)}, bf16[1,1,256,64,128]{4,2,3,1,0:T(8,128)(2,1)}) fusion(f32[1,2,256,64,128]{4,2,3,1,0:T(8,128)S(1)} %bitcast.213, s32[64,128]{1,0:T(8,128)S(1)} %iota_add_fusion, s32[256]{0:T(256)S(1)} %fusion.122), kind=kLoop, calls=%fused_computation.71 | loop fusion | flops 46137344 | bytes 25199616 | tf_op jit(solution)/shard_map/convert.9
  180.7 6.4 copy.202
  187.2 6.4 copy.203
  193.6 7.6 pad_maximum_fusion.4
  201.2 16.4 %copy.204 = bf16[1,2,256,8192]{2,1,0,3:T(2,128)(2,1)} copy(bf16[1,2,256,8192]{2,3,1,0:T(8,128)(2,1)} %pad_maximum_fusion.4) | data formatting | bytes 16777216 | tf_op jit(solution)/shard_map/stack | solution.py:78
  217.6 6.7 all-to-all-start.2
  224.3 12.7 %copy.286 = bf16[1,2,256,8192]{3,2,1,0:T(8,128)(2,1)} copy(bf16[1,2,256,8192]{3,1,2,0:T(2,128)(2,1)} %bitcast.228) | data formatting | bytes 16777216
  237.0 21.0 %copy.183 = bf16[2,256,8192]{1,0,2:T(2,128)(2,1)} copy(bf16[2,256,8192]{2,1,0:T(8,128)(2,1)} %bitcast.222) | data formatting | bytes 16777216 | tf_op jit(solution)/shard_map/reshape | solution.py:157
  258.0 148.7 %all-to-all-done.2 = bf16[1,2,256,8192]{2,1,0,3:T(2,128)(2,1)} async-done(((bf16[1,2,256,8192]{2,1,0,3:T(2,128)(2,1)}), bf16[1,2,256,8192]{2,1,0,3:T(2,128)(2,1)}, u32[]{:S(2)}, u32[]{:S(2)}) %all-to-all-start.2) | async-done | bytes 8388640 | tf_op jit(solution)/shard_map/all_to_all | solution.py:196
  406.7 4.7 all-to-all-start
  413.2 0.8 multiply_sine_fusion.1
  414.0 7.9 copy.205
  421.8 11.9 %copy.206 = bf16[1,2,16,256,512]{4,3,2,1,0:T(8,128)(2,1)} copy(bf16[1,2,16,256,512]{3,4,2,1,0:T(8,128)(2,1)} %bitcast.219) | data formatting | bytes 16777216 | tf_op jit(solution)/shard_map/all_to_all | solution.py:196
  433.7 4.8 fusion.42
  438.5 3.9 fusion.61
  442.4 6.4 pad_maximum_fusion.5
  448.7 14.3 %fusion.14 = f32[2,32,128,512]{3,1,2,0:T(8,128)S(1)} fusion(bf16[2,32,128,512]{3,2,1,0:T(8,128)(2,1)} %pad_maximum_fusion.5, bf16[1,2,32,32]{2,3,1,0:T(8,128)(2,1)S(1)} %get-tuple-element.43, bf16[1,2,32,32]{2,3,1,0:T(8,128)(2,1)S(1)} %get-tuple-element.42), kind=kOutput, calls=%fused_computation.35 | convolution fusion | flops 545263616 | bytes 25174016 | tf_op jit(solution)/shard_map/dikyb,iokx->doxyb/dot_general | solution.py:82
  463.0 19.7 %copy.211 = f32[2,32,128,512]{3,2,1,0:T(8,128)} copy(f32[2,32,128,512]{3,1,2,0:T(8,128)S(1)} %fusion.14) | data formatting | bytes 33554432 | tf_op jit(solution)/shard_map/convert_element_type | solution.py:143
  482.7 9.6 fusion.15
  492.3 8.9 copy.212
  501.2 4.9 reduce_sum.9
  506.2 2.8 copy.213
  509.4 22.4 %reduce.2 = bf16[4096,32]{1,0:T(8,128)(2,1)S(1)} reduce(bf16[4096,1,32]{2,1,0:T(2,128)(2,1)S(1)} %bitcast.229, bf16[]{:T(256)} %broadcast.2052), dimensions={1}, to_apply=%bitcast.198.reduce_sub_computation | reduce | bytes 524290
  531.8 1.7 reshape.1483
  533.5 60.3 %all-to-all-done = bf16[2,256,8192]{1,0,2:T(2,128)(2,1)} async-done(((bf16[2,256,8192]{1,0,2:T(2,128)(2,1)}), bf16[2,256,8192]{1,0,2:T(2,128)(2,1)}, u32[]{:S(2)}, u32[]{:S(2)}) %all-to-all-start) | async-done | bytes 8388640 | tf_op jit(solution)/shard_map/all_to_all | solution.py:158
  593.8 4.8 all-to-all-start.3
  598.7 7.9 copy.184
  606.5 11.9 %copy.185 = bf16[2,16,256,512]{3,2,1,0:T(8,128)(2,1)} copy(bf16[2,16,256,512]{2,3,1,0:T(8,128)(2,1)} %bitcast.220) | data formatting | bytes 16777216 | tf_op jit(solution)/shard_map/all_to_all | solution.py:158
  618.4 14.3 %fusion.36 = f32[1,2,32,128,512]{4,2,3,1,0:T(8,128)S(1)} fusion(bf16[2,32,128,512]{3,2,1,0:T(8,128)(2,1)} %bitcast.216, bf16[1,2,32,32]{2,3,0,1:T(8,128)(2,1)S(1)} %get-tuple-element.45, bf16[1,2,32,32]{2,3,0,1:T(8,128)(2,1)S(1)} %get-tuple-element.44), kind=kOutput, calls=%fused_computation.82 | convolution fusion | flops 536887296 | bytes 25174016 | tf_op jit(solution)/shard_map/dixyb,ioxk->dokyb/dot_general | solution.py:82
  632.7 4.2 fusion.53
  636.9 6.3 pad_maximum_fusion
  643.2 13.8 %fusion.39 = f32[1,2,32,128,512]{4,3,2,1,0:T(8,128)S(1)} fusion(bf16[2,32,128,512]{3,1,2,0:T(8,128)(2,1)} %pad_maximum_fusion, bf16[1,2,128,128]{2,3,0,1:T(8,128)(2,1)S(1)} %get-tuple-element.37, bf16[1,2,128,128]{2,3,0,1:T(8,128)(2,1)S(1)} %get-tuple-element.36), kind=kOutput, calls=%fused_computation.83 | convolution fusion | flops 2147745792 | bytes 25296896 | tf_op jit(solution)/shard_map/dikyb,ioyq->dokqb/dot_general | solution.py:82
  657.0 36.5 %subtract_convert_fusion.5 = (bf16[1,1,32,128,512]{4,3,2,1,0:T(8,128)(2,1)S(1)}, bf16[1,1,32,128,512]{4,3,2,1,0:T(8,128)(2,1)S(1)}) fusion(f32[1,2,32,128,512]{4,3,2,1,0:T(8,128)S(1)} %fusion.39, s32[512]{0:T(512)S(1)} %iota_add_fusion.3, s32[32,128]{1,0:T(8,128)S(1)} %iota_add_fusion.2), kind=kLoop, calls=%fused_computation.79 | loop fusion | flops 46137344 | bytes 25184256 | tf_op jit(solution)/shard_map/convert.49
  693.5 31.1 %copy.190 = bf16[1,1,4096,512]{3,1,0,2:T(2,128)(2,1)S(1)} copy(bf16[1,1,4096,512]{3,2,1,0:T(8,128)(2,1)S(1)} %bitcast.224) | data formatting | bytes 8388608 | tf_op jit(solution)/shard_map/stack | solution.py:78
  724.6 31.1 %copy.191 = bf16[1,1,4096,512]{3,1,0,2:T(2,128)(2,1)S(1)} copy(bf16[1,1,4096,512]{3,2,1,0:T(8,128)(2,1)S(1)} %bitcast.223) | data formatting | bytes 8388608 | tf_op jit(solution)/shard_map/stack | solution.py:78
  755.7 20.3 %pad_maximum_fusion.1 = bf16[1,2,4096,512]{3,1,0,2:T(2,128)(2,1)} fusion(bf16[1,1,4096,512]{3,1,0,2:T(2,128)(2,1)S(1)} %copy.191, bf16[1,1,4096,512]{3,1,0,2:T(2,128)(2,1)S(1)} %copy.190), kind=kLoop, calls=%fused_computation.41 | loop fusion | flops 16777216 | bytes 16777216 | tf_op jit(solution)/shard_map/stack | solution.py:78
  776.0 6.2 all-to-all-start.1
  782.2 1.3 reshape.1484
  783.5 2.1 copy.214
  785.7 1.0 copy.215
  787.3 2.0 collective-permute-start
  789.4 4.4 collective-permute-start.1
  793.8 170.2 %collective-permute-done = bf16[1,16]{1,0:T(2,128)(2,1)S(1)} collective-permute-done((bf16[1,16]{1,0:T(2,128)(2,1)S(1)}, bf16[1,16]{1,0:T(2,128)(2,1)S(1)}, u32[]{:S(2)}, u32[]{:S(2)}) %collective-permute-start) | collective-permute-done | bytes 64 | tf_op jit(solution)/shard_map/ppermute | solution.py:24
  964.1 7.9 dynamic-update-slice.1
  972.3 0.6 convert_element_type.400
  972.9 36.0 %fusion.69 = f32[1,131072]{1,0:T(1,128)} fusion(f32[1,131104]{1,0:T(1,128)S(1)} %convert_element_type.400), kind=kLoop, calls=%fused_computation.105 | loop fusion | flops 4325376 | bytes 17825792 | tf_op jit(solution)/shard_map/div | solution.py:209
  1008.9 15.9 %copy.287 = bf16[1,2,16,256,512]{4,2,1,3,0:T(8,128)(2,1)} copy(bf16[1,2,16,256,512]{4,1,3,2,0:T(2,128)(2,1)} %bitcast.33) | data formatting | bytes 16777216 | tf_op jit(solution)/shard_map/all_to_all | solution.py:179
  1024.7 13.9 %reshape.1466 = bf16[2,256,64,128,1]{3,2,0,1,4:T(8,128)(2,1)} reshape(bf16[1,2,256,16,512]{4,3,1,2,0:T(8,128)(2,1)} %bitcast.221) | data formatting | bytes 16777216 | tf_op jit(solution)/shard_map/reshape.24
  1038.7 5.8 convolution_bitcast_fusion
  1044.5 4.1 fusion.55
  1048.6 6.4 pad_maximum_fusion.2
  1054.9 16.7 %bitcast_convert_fusion.1 = bf16[2,128,256,64]{2,1,3,0:T(8,128)(2,1)} fusion(bf16[2,256,64,128]{3,2,1,0:T(8,128)(2,1)} %pad_maximum_fusion.2, bf16[1,2,128,128]{2,3,0,1:T(8,128)(2,1)S(1)} %get-tuple-element.37, bf16[1,2,128,128]{2,3,0,1:T(8,128)(2,1)S(1)} %get-tuple-element.36), kind=kOutput, calls=%fused_computation.1 | convolution fusion | flops 2151940096 | bytes 16908288 | tf_op jit(solution)/shard_map/dimjy,ioyq->domjq/dot_general | solution.py:82
  1071.7 12.0 %copy.216 = bf16[2,256,8192]{2,1,0:T(8,128)(2,1)} copy(bf16[2,256,8192]{1,2,0:T(8,128)(2,1)} %bitcast.217) | data formatting | bytes 16777216
  (51 shorter events, 4.5 us)
Async XLA Ops:
  217.6 189.1 %all-to-all-start.2 = ((bf16[1,2,256,8192]{2,1,0,3:T(2,128)(2,1)}), bf16[1,2,256,8192]{2,1,0,3:T(2,128)(2,1)}, u32[]{:S(2)}, u32[]{:S(2)}) async-start(bf16[1,2,256,8192]{2,1,0,3:T(2,128)(2,1)} %copy.204), calls=%async_computation.2 | async-start | bytes 16777216 | tf_op jit(solution)/shard_map/all_to_all | solution.py:196
  406.7 187.1 %all-to-all-start = ((bf16[2,256,8192]{1,0,2:T(2,128)(2,1)}), bf16[2,256,8192]{1,0,2:T(2,128)(2,1)}, u32[]{:S(2)}, u32[]{:S(2)}) async-start(bf16[2,256,8192]{1,0,2:T(2,128)(2,1)} %copy.183), calls=%async_computation | async-start | bytes 16777216 | tf_op jit(solution)/shard_map/all_to_all | solution.py:158
  593.8 182.2 %all-to-all-start.3 = ((bf16[16,2,4096]{2,1,0:T(2,128)(2,1)}), bf16[16,2,4096]{2,1,0:T(2,128)(2,1)S(1)}, u32[]{:S(2)}, u32[]{:S(2)}) async-start(bf16[16,2,4096]{2,1,0:T(2,128)(2,1)} %reshape.1483), calls=%async_computation.3 | async-start | bytes 524288 | tf_op jit(solution)/shard_map/all_to_all | solution.py:198
  776.0 188.0 %copy-start = (bf16[1,131104]{1,0:T(2,128)(2,1)S(1)}, bf16[1,131104]{1,0:T(2,128)(2,1)}, u32[]{:S(2)}) copy-start(bf16[1,131104]{1,0:T(2,128)(2,1)} %custom-call) | copy-start | bytes 786628
  776.0 232.9 %all-to-all-start.1 = ((bf16[1,2,4096,512]{3,1,0,2:T(2,128)(2,1)}), bf16[1,2,4096,512]{3,1,0,2:T(2,128)(2,1)}, u32[]{:S(2)}, u32[]{:S(2)}) async-start(bf16[1,2,4096,512]{3,1,0,2:T(2,128)(2,1)} %pad_maximum_fusion.1), calls=%async_computation.1 | async-start | bytes 16777216 | tf_op jit(solution)/shard_map/all_to_all | solution.py:179
  787.3 176.7 %collective-permute-start = (bf16[1,16]{1,0:T(2,128)(2,1)S(1)}, bf16[1,16]{1,0:T(2,128)(2,1)S(1)}, u32[]{:S(2)}, u32[]{:S(2)}) collective-permute-start(bf16[1,16]{1,0:T(2,128)(2,1)S(1)} %get-tuple-element.33), channel_id=1, source_target_pairs={{0,1},{1,2},{2,3},{3,4},{4,5},{5,6},{6,7},{7,8},{8,9},{9,10},{10,1... | collective-permute-start | bytes 104 | tf_op jit(solution)/shard_map/ppermute | solution.py:24
  789.4 182.7 %collective-permute-start.1 = (bf16[1,16]{1,0:T(2,128)(2,1)S(1)}, bf16[1,16]{1,0:T(2,128)(2,1)S(1)}, u32[]{:S(2)}, u32[]{:S(2)}) collective-permute-start(bf16[1,16]{1,0:T(2,128)(2,1)S(1)} %get-tuple-element.32), channel_id=1, source_target_pairs={{1,0},{2,1},{3,2},{4,3},{5,4},{6,5},{7,6},{8,7},{9,8},{10,9},{11,1... | collective-permute-start | bytes 104 | tf_op jit(solution)/shard_map/ppermute | solution.py:27
  1038.7 5.8 copy-start.1
  1038.7 5.8 copy-start.2
where the time goes:
time: 1100 us; the launch traced here: 1080 us
  waiting for transfers between devices  379 us (34%)
  local copies, waits for them, and re-layouts  325 us (30%)
  other arithmetic  266 us (24%)
  matrix products  82.4 us (7%)
  starting transfers between devices  28.9 us (3%)
    ppermute x1, waiting for transfers between devices, padded_2(): lax.ppermute(lax.slice_in_dim(block, block.shape[dim] - width, None, axis...  170 us
    all_to_all x1, waiting for transfers between devices, on_device(): lax.all_to_all(front_part, 'fft', split_axis=3, concat_axis=2, tiled=True)  149 us
    another operation x11, other arithmetic, rotate(): return jnp.stack([real_part, imag_part], axis=1).astype(jnp.bfloat16)  115 us
    another operation x4, local copies, waits for them, and re-layouts, rotate(): return jnp.stack([real_part, imag_part], axis=1).astype(jnp.bfloat16)  90.7 us
    dot_general x8, matrix products, dft_section(): jnp.einsum(einsum_form, values, dft_table(length, direction), preferred_e...  82.4 us
    another operation x14, other arithmetic  75.7 us
    unnamed x17, local copies, waits for them, and re-layouts  66.2 us
    all_to_all x1, waiting for transfers between devices, on_device(): lax.all_to_all(values, 'fft', split_axis=2, concat_axis=1, tiled=True)  60.3 us
  transfers between devices with their start and end apart: 6, of which 3 were waited for; matrix products, arithmetic and copies ran while one was open for 35% of the time, Pallas kernels for 0%

commit v1 on v0

--- a/solution.py
+++ b/solution.py
@@ -3,6 +3,7 @@
 import jax.numpy as jnp
 from jax import lax
 from jax.sharding import PartitionSpec as P
+from jax.lax import all_to_all, psum
 
 ROWS_OUTER = 32
 ROWS_INNER = 128
@@ -193,7 +194,9 @@
     row_start = device_index * row_local
     trial_total = dm_index.shape[0]
     front_part = chirp_front(spectrum_in, grid_steps, row_start, row_local)
-    moved = lax.all_to_all(front_part, "fft", split_axis=3, concat_axis=2, tiled=True)
+    moved = jnp.concatenate(
+        all_to_all(jnp.stack(jnp.split(front_part, psum(1, axis_name="fft"), 3), 0), "fft", 0, 0), 2
+    )
     pieces = finish_rows(moved)
     decimated_power = lax.all_to_all(
         detect(pieces).astype(jnp.bfloat16), "fft", split_axis=1, concat_axis=2, tiled=True

time: 1100 us -> 1090 us (level)
  local copies, waits for them, and re-layouts: 325 us -> 303 us
    all_to_all x2 -> x0, local copies, waits for them, and re-layouts: 19.7 us -> none  [on_device(): lax.all_to_all(front_part, 'fft', split_axis=3, concat_axis=2, tiled=True)]
    another operation x4 -> x3, local copies, waits for them, and re-layouts: 90.7 us -> 74.4 us  [rotate(): return jnp.stack([real_part, imag_part], axis=1).astype(jnp.bfloat16)]
    unnamed x2 -> x17, other arithmetic: 22.4 us -> 36.2 us
    reshape x0 -> x1, local copies, waits for them, and re-layouts: none -> 11.9 us  [on_device(): jnp.concatenate(all_to_all(jnp.stack(jnp.split(front_part, psum(1, axis_n...]
    another operation x11 -> x10, other arithmetic: 115 us -> 108 us  [rotate(): return jnp.stack([real_part, imag_part], axis=1).astype(jnp.bfloat16)]
    unnamed x17 -> x23, local copies, waits for them, and re-layouts: 66.2 us -> 68 us
    another operation x14 -> x15, other arithmetic: 75.7 us -> 76.6 us
where the time goes in v1:
time: 1090 us; the launch traced here: 1080 us
  waiting for transfers between devices  386 us (35%)
  local copies, waits for them, and re-layouts  303 us (28%)
  other arithmetic  274 us (25%)
  matrix products  82.4 us (8%)
  starting transfers between devices  28.9 us (3%)
    ppermute x1, waiting for transfers between devices, padded_2(): lax.ppermute(lax.slice_in_dim(block, block.shape[dim] - width, None, axis...  170 us
    all_to_all x1, waiting for transfers between devices, on_device(): all_to_all(jnp.stack(jnp.split(front_part, psum(1, axis_name='fft'), 3),...  149 us
    another operation x10, other arithmetic, rotate(): return jnp.stack([real_part, imag_part], axis=1).astype(jnp.bfloat16)  108 us
    dot_general x8, matrix products, dft_section(): jnp.einsum(einsum_form, values, dft_table(length, direction), preferred_e...  82.4 us
    another operation x14, other arithmetic  75.7 us
    another operation x3, local copies, waits for them, and re-layouts, rotate(): return jnp.stack([real_part, imag_part], axis=1).astype(jnp.bfloat16)  74.4 us
    unnamed x23, local copies, waits for them, and re-layouts  68 us
    all_to_all x1, waiting for transfers between devices, on_device(): lax.all_to_all(values, 'fft', split_axis=2, concat_axis=1, tiled=True)  67 us
  transfers between devices with their start and end apart: 6, of which 3 were waited for; matrix products, arithmetic and copies ran while one was open for 35% of the time, Pallas kernels for 0%

profile of v1, /device:TPU:16, one launch (start us, length us, event | category | flops | bytes accessed | tf_op | source)
XLA Modules:
  0.0 1076.3 jit_solution(1146254545277586247)
XLA Ops:
  2.5 11.9 %copy.192 = bf16[2,256,8192]{1,2,0:T(8,128)(2,1)} copy(bf16[2,256,8192]{2,1,0:T(8,128)(2,1)} %param.4) | data formatting | bytes 16777216 | tf_op args[1]
  14.4 11.6 %fusion.146 = (f32[1,1,256,64,128]{2,4,3,1,0:T(8,128)}, f32[1,1,256,64,128]{2,4,3,1,0:T(8,128)}) fusion(bf16[1,2,256,64,128]{2,4,3,1,0:T(8,128)(2,1)} %bitcast.276), kind=kLoop, calls=%fused_computation.349 | loop fusion | bytes 33554432 | tf_op jit(solution)/shard_map/slice | solution.py:77
  26.0 9.1 copy.236
  35.0 9.0 copy.237
  44.0 41.0 %fusion.57 = (bf16[1,256,64,128]{3,1,0,2:T(8,128)(2,1)S(1)}, bf16[1,256,64,128]{3,1,0,2:T(8,128)(2,1)S(1)}) fusion(f32[1,1,256,64,128]{4,2,3,1,0:T(8,128)} %copy.237, f32[1,1,256,64,128]{4,2,3,1,0:T(8,128)} %copy.236, f32[64,128]{1,0:T(8,128)S(1)} %fusion.114, s32[64,128]{1,0:T(8,128)S(1)} %iota_add_fusion.1, s32[256]{0:T(256)S(1)} %fusion.139, ...), kind=kLoop, calls=%fused_computation.121 | loop fusion | flops 77594624 | bytes 25233412 | tf_op jit(solution)/shard_map/stack | solution.py:79
  85.0 7.0 fusion.47
  92.1 8.8 fusion.59
  100.9 6.3 pad_maximum_fusion.3
  107.2 12.2 %copy.198 = bf16[2,256,64,128]{3,2,0,1:T(8,128)(2,1)} copy(bf16[2,256,64,128]{1,3,2,0:T(8,128)(2,1)} %pad_maximum_fusion.3) | data formatting | bytes 16777216 | tf_op jit(solution)/shard_map/stack | solution.py:79
  119.5 5.8 fusion.48
  125.2 18.3 %copy.281 = f32[2,64,256,128]{3,2,1,0:T(8,128)S(1)} copy(f32[2,64,256,128]{3,1,2,0:T(8,128)S(1)} %fusion.48) | data formatting | bytes 33554432 | tf_op jit(solution)/shard_map/dimjy,iojx->domxy/dot_general | solution.py:83
  143.6 37.2 %subtract_convert_fusion.1 = (bf16[1,1,256,64,128]{4,2,3,1,0:T(8,128)(2,1)}, bf16[1,1,256,64,128]{4,2,3,1,0:T(8,128)(2,1)}) fusion(f32[1,2,256,64,128]{4,2,3,1,0:T(8,128)S(1)} %bitcast.277, s32[64,128]{1,0:T(8,128)S(1)} %iota_add_fusion, s32[256]{0:T(256)S(1)} %fusion.139), kind=kLoop, calls=%fused_computation.100 | loop fusion | flops 46137344 | bytes 25199616 | tf_op jit(solution)/shard_map/convert.9
  180.8 6.4 copy.200
  187.2 6.4 copy.201
  193.5 2.1 bitcast_dynamic-update-slice_fusion.14
  196.1 1.3 copy-done.1
  203.2 0.9 bitcast_dynamic-update-slice_fusion.6
  206.5 0.9 bitcast_dynamic-update-slice_fusion.2
  208.2 0.9 bitcast_dynamic-update-slice_fusion
  209.9 6.7 all-to-all-start.2
  216.6 12.7 %copy.282 = bf16[1,2,256,8192]{3,2,1,0:T(8,128)(2,1)} copy(bf16[1,2,256,8192]{3,1,2,0:T(2,128)(2,1)} %bitcast.289) | data formatting | bytes 16777216
  229.3 21.0 %copy.181 = bf16[2,256,8192]{1,0,2:T(2,128)(2,1)} copy(bf16[2,256,8192]{2,1,0:T(8,128)(2,1)} %bitcast.285) | data formatting | bytes 16777216 | tf_op jit(solution)/shard_map/reshape | solution.py:158
  250.3 148.7 %all-to-all-done.2 = bf16[16,1,2,256,512]{3,4,2,1,0:T(8,128)(2,1)} async-done(((bf16[16,1,2,256,512]{3,4,2,1,0:T(8,128)(2,1)}), bf16[16,1,2,256,512]{3,4,2,1,0:T(8,128)(2,1)}, u32[]{:S(2)}, u32[]{:S(2)}) %all-to-all-start.2) | async-done | bytes 8388640 | tf_op jit(solution)/shard_map/all_to_all | solution.py:198
  399.0 4.7 all-to-all-start
  407.4 11.9 %copy.202 = bf16[1,2,16,256,512]{4,3,2,1,0:T(8,128)(2,1)} copy(bf16[1,2,16,256,512]{3,4,1,0,2:T(8,128)(2,1)} %bitcast.97) | data formatting | bytes 16777216 | tf_op jit(solution)/shard_map/reshape | solution.py:197
  419.3 4.8 fusion.42
  424.1 3.9 fusion.61
  428.0 6.4 pad_maximum_fusion.4
  434.3 14.3 %fusion.14 = f32[2,32,128,512]{3,1,2,0:T(8,128)S(1)} fusion(bf16[2,32,128,512]{3,2,1,0:T(8,128)(2,1)} %pad_maximum_fusion.4, bf16[1,2,32,32]{2,3,1,0:T(8,128)(2,1)S(1)} %get-tuple-element.43, bf16[1,2,32,32]{2,3,1,0:T(8,128)(2,1)S(1)} %get-tuple-element.42), kind=kOutput, calls=%fused_computation.65 | convolution fusion | flops 545263616 | bytes 25174016 | tf_op jit(solution)/shard_map/dikyb,iokx->doxyb/dot_general | solution.py:83
  448.6 19.7 %copy.207 = f32[2,32,128,512]{3,2,1,0:T(8,128)} copy(f32[2,32,128,512]{3,1,2,0:T(8,128)S(1)} %fusion.14) | data formatting | bytes 33554432 | tf_op jit(solution)/shard_map/convert_element_type | solution.py:144
  468.2 9.6 fusion.15
  477.8 9.0 copy.208
  486.8 4.9 reduce_sum.9
  491.8 2.8 copy.209
  495.0 22.4 %reduce.2 = bf16[4096,32]{1,0:T(8,128)(2,1)S(1)} reduce(bf16[4096,1,32]{2,1,0:T(2,128)(2,1)S(1)} %bitcast.290, bf16[]{:T(256)} %broadcast.2052), dimensions={1}, to_apply=%bitcast.230.reduce_sub_computation | reduce | bytes 524290
  517.4 1.7 reshape.1485
  519.1 67.0 %all-to-all-done = bf16[2,256,8192]{1,0,2:T(2,128)(2,1)} async-done(((bf16[2,256,8192]{1,0,2:T(2,128)(2,1)}), bf16[2,256,8192]{1,0,2:T(2,128)(2,1)}, u32[]{:S(2)}, u32[]{:S(2)}) %all-to-all-start) | async-done | bytes 8388640 | tf_op jit(solution)/shard_map/all_to_all | solution.py:159
  586.1 4.8 all-to-all-start.3
  591.0 7.9 copy.182
  598.8 11.9 %copy.183 = bf16[2,16,256,512]{3,2,1,0:T(8,128)(2,1)} copy(bf16[2,16,256,512]{2,3,1,0:T(8,128)(2,1)} %bitcast.283) | data formatting | bytes 16777216 | tf_op jit(solution)/shard_map/all_to_all | solution.py:159
  610.7 14.3 %fusion.36 = f32[1,2,32,128,512]{4,2,3,1,0:T(8,128)S(1)} fusion(bf16[2,32,128,512]{3,2,1,0:T(8,128)(2,1)} %bitcast.280, bf16[1,2,32,32]{2,3,0,1:T(8,128)(2,1)S(1)} %copy-done.3, bf16[1,2,32,32]{2,3,0,1:T(8,128)(2,1)S(1)} %get-tuple-element.44), kind=kOutput, calls=%fused_computation.111 | convolution fusion | flops 536887296 | bytes 25174016 | tf_op jit(solution)/shard_map/dixyb,ioxk->dokyb/dot_general | solution.py:83
  625.0 4.2 fusion.53
  629.2 6.3 pad_maximum_fusion
  635.5 13.8 %fusion.39 = f32[1,2,32,128,512]{4,3,2,1,0:T(8,128)S(1)} fusion(bf16[2,32,128,512]{3,1,2,0:T(8,128)(2,1)} %pad_maximum_fusion, bf16[1,2,128,128]{2,3,0,1:T(8,128)(2,1)S(1)} %get-tuple-element.37, bf16[1,2,128,128]{2,3,0,1:T(8,128)(2,1)S(1)} %get-tuple-element.36), kind=kOutput, calls=%fused_computation.112 | convolution fusion | flops 2147745792 | bytes 25296896 | tf_op jit(solution)/shard_map/dikyb,ioyq->dokqb/dot_general | solution.py:83
  649.4 36.5 %subtract_convert_fusion.5 = (bf16[1,1,32,128,512]{4,3,2,1,0:T(8,128)(2,1)S(1)}, bf16[1,1,32,128,512]{4,3,2,1,0:T(8,128)(2,1)S(1)}) fusion(f32[1,2,32,128,512]{4,3,2,1,0:T(8,128)S(1)} %fusion.39, s32[512]{0:T(512)S(1)} %copy-done.5, s32[32,128]{1,0:T(8,128)S(1)} %copy-done.4), kind=kLoop, calls=%fused_computation.108 | loop fusion | flops 46137344 | bytes 25184256 | tf_op jit(solution)/shard_map/convert.49
  685.9 31.1 %copy.188 = bf16[1,1,4096,512]{3,1,0,2:T(2,128)(2,1)S(1)} copy(bf16[1,1,4096,512]{3,2,1,0:T(8,128)(2,1)S(1)} %bitcast.287) | data formatting | bytes 8388608 | tf_op jit(solution)/shard_map/stack | solution.py:79
  717.0 31.1 %copy.189 = bf16[1,1,4096,512]{3,1,0,2:T(2,128)(2,1)S(1)} copy(bf16[1,1,4096,512]{3,2,1,0:T(8,128)(2,1)S(1)} %bitcast.286) | data formatting | bytes 8388608 | tf_op jit(solution)/shard_map/stack | solution.py:79
  748.1 20.3 %pad_maximum_fusion.1 = bf16[1,2,4096,512]{3,1,0,2:T(2,128)(2,1)} fusion(bf16[1,1,4096,512]{3,1,0,2:T(2,128)(2,1)S(1)} %copy.189, bf16[1,1,4096,512]{3,1,0,2:T(2,128)(2,1)S(1)} %copy.188), kind=kLoop, calls=%fused_computation.71 | loop fusion | flops 16777216 | bytes 16777216 | tf_op jit(solution)/shard_map/stack | solution.py:79
  768.4 6.2 all-to-all-start.1
  774.5 1.3 reshape.1486
  775.9 2.1 copy.210
  778.0 1.0 copy.211
  779.7 2.0 collective-permute-start
  781.7 4.4 collective-permute-start.1
  786.2 170.2 %collective-permute-done = bf16[1,16]{1,0:T(2,128)(2,1)S(1)} collective-permute-done((bf16[1,16]{1,0:T(2,128)(2,1)S(1)}, bf16[1,16]{1,0:T(2,128)(2,1)S(1)}, u32[]{:S(2)}, u32[]{:S(2)}) %collective-permute-start) | collective-permute-done | bytes 64 | tf_op jit(solution)/shard_map/ppermute | solution.py:25
  956.5 7.9 dynamic-update-slice.1
  965.2 36.0 %fusion.84 = f32[1,131072]{1,0:T(1,128)} fusion(f32[1,131104]{1,0:T(1,128)S(1)} %convert_element_type.400), kind=kLoop, calls=%fused_computation.149 | loop fusion | flops 4325376 | bytes 17825792 | tf_op jit(solution)/shard_map/div | solution.py:212
  1001.2 15.9 %copy.283 = bf16[1,2,16,256,512]{4,2,1,3,0:T(8,128)(2,1)} copy(bf16[1,2,16,256,512]{4,1,3,2,0:T(2,128)(2,1)} %bitcast.33) | data formatting | bytes 16777216 | tf_op jit(solution)/shard_map/all_to_all | solution.py:180
  1017.1 13.9 %reshape.1468 = bf16[2,256,64,128,1]{3,2,0,1,4:T(8,128)(2,1)} reshape(bf16[1,2,256,16,512]{4,3,1,2,0:T(8,128)(2,1)} %bitcast.284) | data formatting | bytes 16777216 | tf_op jit(solution)/shard_map/reshape.24
  1031.0 5.8 convolution_bitcast_fusion
  1036.8 4.1 fusion.55
  1040.9 6.4 pad_maximum_fusion.2
  1047.3 16.7 %bitcast_convert_fusion.1 = bf16[2,128,256,64]{2,1,3,0:T(8,128)(2,1)} fusion(bf16[2,256,64,128]{3,2,1,0:T(8,128)(2,1)} %pad_maximum_fusion.2, bf16[1,2,128,128]{2,3,0,1:T(8,128)(2,1)S(1)} %get-tuple-element.37, bf16[1,2,128,128]{2,3,0,1:T(8,128)(2,1)S(1)} %get-tuple-element.36), kind=kOutput, calls=%fused_computation.31 | convolution fusion | flops 2151940096 | bytes 16908288 | tf_op jit(solution)/shard_map/dimjy,ioyq->domjq/dot_general | solution.py:83
  1064.0 12.0 %copy.212 = bf16[2,256,8192]{2,1,0:T(8,128)(2,1)} copy(bf16[2,256,8192]{1,2,0:T(8,128)(2,1)} %bitcast.281) | data formatting | bytes 16777216
  (70 shorter events, 17.4 us)
Async XLA Ops:
  193.5 2.5 copy-start
  193.5 3.8 copy-start.1
  209.9 189.1 %all-to-all-start.2 = ((bf16[16,1,2,256,512]{3,4,2,1,0:T(8,128)(2,1)}), bf16[16,1,2,256,512]{3,4,2,1,0:T(8,128)(2,1)}, u32[]{:S(2)}, u32[]{:S(2)}) async-start(bf16[16,1,2,256,512]{3,4,2,1,0:T(8,128)(2,1)} %fusion.86), calls=%async_computation.2 | async-start | bytes 16777216 | tf_op jit(solution)/shard_map/all_to_all | solution.py:198
  399.0 187.1 %all-to-all-start = ((bf16[2,256,8192]{1,0,2:T(2,128)(2,1)}), bf16[2,256,8192]{1,0,2:T(2,128)(2,1)}, u32[]{:S(2)}, u32[]{:S(2)}) async-start(bf16[2,256,8192]{1,0,2:T(2,128)(2,1)} %copy.181), calls=%async_computation | async-start | bytes 16777216 | tf_op jit(solution)/shard_map/all_to_all | solution.py:159
  586.1 182.2 %all-to-all-start.3 = ((bf16[16,2,4096]{2,1,0:T(2,128)(2,1)}), bf16[16,2,4096]{2,1,0:T(2,128)(2,1)S(1)}, u32[]{:S(2)}, u32[]{:S(2)}) async-start(bf16[16,2,4096]{2,1,0:T(2,128)(2,1)} %reshape.1485), calls=%async_computation.3 | async-start | bytes 524288 | tf_op jit(solution)/shard_map/all_to_all | solution.py:201
  598.8 11.9 %copy-start.3 = (bf16[1,2,32,32]{2,3,0,1:T(8,128)(2,1)S(1)}, bf16[1,2,32,32]{2,3,0,1:T(8,128)(2,1)}, u32[]{:S(2)}) copy-start(bf16[1,2,32,32]{2,3,0,1:T(8,128)(2,1)} %get-tuple-element.45) | copy-start | bytes 12292
  635.5 13.8 %copy-start.4 = (s32[32,128]{1,0:T(8,128)S(1)}, s32[32,128]{1,0:T(8,128)}, u32[]{:S(2)}) copy-start(s32[32,128]{1,0:T(8,128)} %iota_add_fusion.2) | copy-start | bytes 49156
  635.5 13.8 %copy-start.5 = (s32[512]{0:T(512)S(1)}, s32[512]{0:T(512)}, u32[]{:S(2)}) copy-start(s32[512]{0:T(512)} %iota_add_fusion.3) | copy-start | bytes 6148
  768.4 188.0 %copy-start.2 = (bf16[1,131104]{1,0:T(2,128)(2,1)S(1)}, bf16[1,131104]{1,0:T(2,128)(2,1)}, u32[]{:S(2)}) copy-start(bf16[1,131104]{1,0:T(2,128)(2,1)} %custom-call) | copy-start | bytes 786628
  768.4 232.9 %all-to-all-start.1 = ((bf16[1,2,4096,512]{3,1,0,2:T(2,128)(2,1)}), bf16[1,2,4096,512]{3,1,0,2:T(2,128)(2,1)}, u32[]{:S(2)}, u32[]{:S(2)}) async-start(bf16[1,2,4096,512]{3,1,0,2:T(2,128)(2,1)} %pad_maximum_fusion.1), calls=%async_computation.1 | async-start | bytes 16777216 | tf_op jit(solution)/shard_map/all_to_all | solution.py:180
  779.7 176.7 %collective-permute-start = (bf16[1,16]{1,0:T(2,128)(2,1)S(1)}, bf16[1,16]{1,0:T(2,128)(2,1)S(1)}, u32[]{:S(2)}, u32[]{:S(2)}) collective-permute-start(bf16[1,16]{1,0:T(2,128)(2,1)S(1)} %get-tuple-element.33), channel_id=1, source_target_pairs={{0,1},{1,2},{2,3},{3,4},{4,5},{5,6},{6,7},{7,8},{8,9},{9,10},{10,1... | collective-permute-start | bytes 104 | tf_op jit(solution)/shard_map/ppermute | solution.py:25
  781.7 182.7 %collective-permute-start.1 = (bf16[1,16]{1,0:T(2,128)(2,1)S(1)}, bf16[1,16]{1,0:T(2,128)(2,1)S(1)}, u32[]{:S(2)}, u32[]{:S(2)}) collective-permute-start(bf16[1,16]{1,0:T(2,128)(2,1)S(1)} %get-tuple-element.32), channel_id=1, source_target_pairs={{1,0},{2,1},{3,2},{4,3},{5,4},{6,5},{7,6},{8,7},{9,8},{10,9},{11,1... | collective-permute-start | bytes 104 | tf_op jit(solution)/shard_map/ppermute | solution.py:28
